TPU v7x, 256 devices: a whole 4x4x8 slice. The times are simulated.
256 devices in a mesh: row: 32 (over y, z), col: 8 (over x, core).
Axes of the slice: x: 4, y: 4, z: 8, core: 2. Of those that a mesh axis runs over, the one named last changes fastest.
Arguments:
- eigvecs: float32 [131072, 1024], P('row', 'col'), may hold values from -6 to 6
- reflectors: float32 [4, 131072, 256], P(None, ('row', 'col'))
- factors: float32 [4, 256, 256], replicated, as said below
Outputs:
- transformed: float32 [131072, 1024], P('row', 'col')
Inputs may be any that keep to these rules, and one draw needn't show every extreme that they name: Each factors[k] is upper triangular with a positive diagonal.
All inputs are finite; a program needn't handle non-finite values.
Results may differ from a plain program's by a relative error of at most 0.00012.
Values sent between devices are 32-bit elements; how exact they have to be, the bound alone decides.
A program may use at most 128 MiB of HBM per device.

v0:
```python
import jax
import jax.numpy as jnp
from jax import lax
from jax.sharding import Mesh
from jax.sharding import PartitionSpec as P

COL = ("col_0", "col_1")
ROW_COL = ("row", "col_0", "col_1")


def copy_for_each(x, axis):
    copies = jnp.broadcast_to(x, (lax.axis_size(axis), *x.shape))
    return lax.all_to_all(copies, axis, split_axis=0, concat_axis=0, tiled=True)


def joined_along(tiles, dim):
    dims = list(tiles.shape[1:])
    dims[dim] *= tiles.shape[0]
    return jnp.moveaxis(tiles, 0, dim).reshape(dims)


def whole_of(x, axes, dim):
    far, near = axes
    leading = copy_for_each(x, far)
    tiles = jnp.swapaxes(copy_for_each(leading, near), 0, 1)
    return joined_along(tiles.reshape(-1, *x.shape), dim)


def padded_to(lines, peers):
    spare = -lines.shape[0] % peers
    if not spare:
        return lines
    return jnp.concatenate([lines, jnp.zeros((spare, *lines.shape[1:]), lines.dtype)])


def gathered_copies(x, axis, dim):
    return joined_along(copy_for_each(x, axis), dim)


def split_up(x, dim, peers):
    dims = x.shape
    tiles = x.reshape(*dims[:dim], peers, dims[dim] // peers, *dims[dim + 1 :])
    return jnp.moveaxis(tiles, dim, 0)


def summed_on_arrival(x, axis, dim):
    tiles = split_up(x, dim, lax.axis_size(axis))
    arrived = lax.all_to_all(tiles, axis, split_axis=0, concat_axis=0, tiled=True)
    return arrived.sum(axis=0)


def total_of(x, axes):
    lines = x.reshape(-1, x.shape[-1])
    padded = padded_to(lines, lax.axis_size(axes))
    whole = gathered_copies(summed_on_arrival(padded, axes, 0), axes, 0)
    return lax.slice_in_dim(whole, 0, len(lines)).reshape(x.shape)


def product(left, right):
    return jnp.dot(left, right, precision=lax.Precision.HIGHEST, preferred_element_type=jnp.float32)


def inner(left, right):
    return lax.dot_general(
        left,
        right,
        (((0,), (0,)), ((), ())),
        precision=lax.Precision.HIGHEST,
        preferred_element_type=jnp.float32,
    )


def keep_same(parts):
    return parts


def apply_panels(field, factors, fetch, reduce_value, spread):
    panels = factors.shape[0]
    for index in range(panels):
        vectors = fetch(index)
        sums = reduce_value((inner(vectors, field),))
        coeffs = product(factors[index], sums[0])
        field = field - product(vectors, spread((coeffs,))[0])
    return field


def body(eigvecs, reflectors, factors):

    def fetch(index):
        return whole_of(reflectors[index], ("col_0", "col_1"), 0)

    def reduce_value(parts):
        return jax.tree.map(lambda part: total_of(part, "row"), parts)

    return apply_panels(eigvecs, factors, fetch, reduce_value, keep_same)


def solution(mesh):
    split = Mesh(mesh.devices.reshape(mesh.shape["row"], 4, 2), ("row", "col_0", "col_1"))
    in_specs = (P("row", COL), P(None, ROW_COL, None), P())
    out_specs = P("row", COL)
    return jax.shard_map(body, mesh=split, in_specs=in_specs, out_specs=out_specs, check_vma=False)
```

profile of v0, /device:TPU:1, one launch (start us, length us, event | category | flops | bytes accessed | tf_op | source)
XLA Modules:
  0.0 320.7 jit_solution(18105307061436955398)
XLA Ops:
  2.1 30.0 %all_to_all.80 = f32[4,512,256]{1,2,0:T(8,128)S(1)} all-to-all(f32[4,512,256]{1,2,0:T(8,128)S(1)} %broadcast_in_dim.36), channel_id=1, replica_groups=mesh['row'=32,'col_0'=4,'col_1'=2] {'col_0'}, dimensions={0} | all-to-all | bytes 4194304 | tf_op jit(solution)/shard_map/all_to_all | solution.py:13
  34.0 9.7 %all_to_all.81 = f32[2,4,512,256]{2,1,3,0:T(4,128)} all-to-all(f32[2,4,512,256]{2,1,3,0:T(4,128)S(1)} %broadcast_in_dim.37), channel_id=1, replica_groups=mesh['row'=32,'col_0'=4,'col_1'=2] {'col_1'}, dimensions={0} | all-to-all | bytes 8388608 | tf_op jit(solution)/shard_map/all_to_all | solution.py:13
  45.2 4.5 %all-to-all-start.4 = ((f32[4,512,256]{2,1,0:T(8,128)}), f32[4,512,256]{2,1,0:T(8,128)}, u32[]{:S(2)}, u32[]{:S(2)}) async-start(f32[4,512,256]{2,1,0:T(8,128)} %broadcast_in_dim.39), calls=%async_computation.4 | async-start | bytes 4194304 | tf_op jit(solution)/shard_map/all_to_all | solution.py:13
  49.7 5.3 %copy.25 = f32[2,4,512,256]{3,2,0,1:T(8,128)} copy(f32[2,4,512,256]{2,1,3,0:T(4,128)} %all_to_all.81) | data formatting | bytes 8388608 | tf_op jit(solution)/shard_map/all_to_all | solution.py:13
  55.0 5.8 %copy.26 = f32[256,4096]{1,0:T(8,128)} copy(f32[256,4096]{0,1:T(8,128)} %bitcast.95) | data formatting | bytes 8388608 | tf_op jit(solution)/shard_map/dot_general | solution.py:64
  60.8 5.9 %fusion.4 = f32[32,8,128]{2,1,0:T(8,128)S(1)} fusion(f32[256,4096]{1,0:T(8,128)} %copy.26, f32[4096,128]{1,0:T(8,128)S(1)} %copy-done.8), kind=kOutput, calls=%fused_computation.8 | convolution fusion | flops 1610612736 | bytes 6422528 | tf_op jit(solution)/shard_map/dot_general | solution.py:64
  66.7 9.1 %all-to-all-done.4 = f32[4,512,256]{2,1,0:T(8,128)} async-done(((f32[4,512,256]{2,1,0:T(8,128)}), f32[4,512,256]{2,1,0:T(8,128)}, u32[]{:S(2)}, u32[]{:S(2)}) %all-to-all-start.4) | async-done | bytes 2097184 | tf_op jit(solution)/shard_map/all_to_all | solution.py:13
  75.8 20.2 %all_to_all.82 = f32[32,8,128]{2,1,0:T(8,128)S(1)} all-to-all(f32[32,8,128]{2,1,0:T(8,128)S(1)} %fusion.4), channel_id=1, replica_groups=mesh['row'=32,'col_0'=4,'col_1'=2] {'row'}, dimensions={0} | all-to-all | bytes 262144 | tf_op jit(solution)/shard_map/all_to_all | solution.py:48
  96.0 3.9 %broadcast_in_dim.40 = f32[2,4,512,256]{3,2,1,0:T(8,128)} broadcast(f32[4,512,256]{2,1,0:T(8,128)} %all-to-all-done.4), dimensions={1,2,3} | broadcast | bytes 6291456 | tf_op jit(solution)/shard_map/broadcast_in_dim | solution.py:12
  99.9 8.3 %all-to-all-start.5 = ((f32[2,4,512,256]{3,2,1,0:T(8,128)}), f32[2,4,512,256]{3,2,1,0:T(8,128)}, u32[]{:S(2)}, u32[]{:S(2)}) async-start(f32[2,4,512,256]{3,2,1,0:T(8,128)} %broadcast_in_dim.40), calls=%async_computation.5 | async-start | bytes 8388608 | tf_op jit(solution)/shard_map/all_to_all | solution.py:13
  108.3 4.1 %all-to-all-done.5 = f32[2,4,512,256]{3,2,1,0:T(8,128)} async-done(((f32[2,4,512,256]{3,2,1,0:T(8,128)}), f32[2,4,512,256]{3,2,1,0:T(8,128)}, u32[]{:S(2)}, u32[]{:S(2)}) %all-to-all-start.5) | async-done | bytes 4194336 | tf_op jit(solution)/shard_map/all_to_all | solution.py:13
  112.4 12.3 %all_to_all.83 = f32[32,8,128]{2,1,0:T(8,128)S(1)} all-to-all(f32[32,8,128]{2,1,0:T(8,128)S(1)} %broadcast_in_dim.38), channel_id=1, replica_groups=mesh['row'=32,'col_0'=4,'col_1'=2] {'row'}, dimensions={0} | all-to-all | bytes 262144 | tf_op jit(solution)/shard_map/all_to_all | solution.py:13
  126.2 4.6 %all-to-all-start.8 = ((f32[4,512,256]{2,1,0:T(8,128)}), f32[4,512,256]{2,1,0:T(8,128)}, u32[]{:S(2)}, u32[]{:S(2)}) async-start(f32[4,512,256]{2,1,0:T(8,128)} %broadcast_in_dim.42), calls=%async_computation.8 | async-start | bytes 4194304 | tf_op jit(solution)/shard_map/all_to_all | solution.py:13
  138.1 4.3 %fusion.3 = f32[4096,128]{0,1:T(8,128)S(1)} fusion(f32[4096,128]{0,1:T(8,128)S(1)} %copy-done.9, f32[128,256]{1,0:T(8,128)S(1)} %fusion.13, f32[4096,256]{1,0:T(8,128)S(1)} %bitcast.96), kind=kOutput, calls=%fused_computation.7 | convolution fusion | flops 1611137024 | bytes 8519680 | tf_op jit(solution)/shard_map/dot_general | solution.py:60
  144.7 10.4 %all-to-all-done.8 = f32[4,512,256]{2,1,0:T(8,128)} async-done(((f32[4,512,256]{2,1,0:T(8,128)}), f32[4,512,256]{2,1,0:T(8,128)}, u32[]{:S(2)}, u32[]{:S(2)}) %all-to-all-start.8) | async-done | bytes 2097184 | tf_op jit(solution)/shard_map/all_to_all | solution.py:13
  155.1 14.3 %all_to_all.84 = f32[32,8,128]{2,1,0:T(8,128)S(1)} all-to-all(f32[32,8,128]{2,1,0:T(8,128)S(1)} %bitcast.99), channel_id=1, replica_groups=mesh['row'=32,'col_0'=4,'col_1'=2] {'row'}, dimensions={0} | all-to-all | bytes 262144 | tf_op jit(solution)/shard_map/all_to_all | solution.py:48
  173.3 9.1 %all-to-all-start.9 = ((f32[2,4,512,256]{3,2,1,0:T(8,128)}), f32[2,4,512,256]{3,2,1,0:T(8,128)}, u32[]{:S(2)}, u32[]{:S(2)}) async-start(f32[2,4,512,256]{3,2,1,0:T(8,128)} %broadcast_in_dim.43), calls=%async_computation.9 | async-start | bytes 8388608 | tf_op jit(solution)/shard_map/all_to_all | solution.py:13
  182.4 4.1 %all-to-all-done.9 = f32[2,4,512,256]{3,2,1,0:T(8,128)} async-done(((f32[2,4,512,256]{3,2,1,0:T(8,128)}), f32[2,4,512,256]{3,2,1,0:T(8,128)}, u32[]{:S(2)}, u32[]{:S(2)}) %all-to-all-start.9) | async-done | bytes 4194336 | tf_op jit(solution)/shard_map/all_to_all | solution.py:13
  186.5 12.3 %all_to_all.85 = f32[32,8,128]{2,1,0:T(8,128)S(1)} all-to-all(f32[32,8,128]{2,1,0:T(8,128)S(1)} %broadcast_in_dim.41), channel_id=1, replica_groups=mesh['row'=32,'col_0'=4,'col_1'=2] {'row'}, dimensions={0} | all-to-all | bytes 262144 | tf_op jit(solution)/shard_map/all_to_all | solution.py:13
  200.4 4.7 %all-to-all-start.12 = ((f32[4,512,256]{2,1,0:T(8,128)}), f32[4,512,256]{2,1,0:T(8,128)}, u32[]{:S(2)}, u32[]{:S(2)}) async-start(f32[4,512,256]{2,1,0:T(8,128)} %broadcast_in_dim.45), calls=%async_computation.12 | async-start | bytes 4194304 | tf_op jit(solution)/shard_map/all_to_all | solution.py:13
  208.9 4.4 %fusion.2 = f32[4096,128]{0,1:T(8,128)S(1)} fusion(f32[4096,128]{0,1:T(8,128)S(1)} %fusion.3, f32[128,256]{1,0:T(8,128)S(1)} %fusion.11, f32[4096,256]{1,0:T(8,128)S(1)} %bitcast.92), kind=kOutput, calls=%fused_computation.5 | convolution fusion | flops 1611137024 | bytes 8519680 | tf_op jit(solution)/shard_map/dot_general | solution.py:60
  216.8 12.4 %all-to-all-done.12 = f32[4,512,256]{2,1,0:T(8,128)} async-done(((f32[4,512,256]{2,1,0:T(8,128)}), f32[4,512,256]{2,1,0:T(8,128)}, u32[]{:S(2)}, u32[]{:S(2)}) %all-to-all-start.12) | async-done | bytes 2097184 | tf_op jit(solution)/shard_map/all_to_all | solution.py:13
  229.3 14.3 %all_to_all.86 = f32[32,8,128]{2,1,0:T(8,128)S(1)} all-to-all(f32[32,8,128]{2,1,0:T(8,128)S(1)} %bitcast.100), channel_id=1, replica_groups=mesh['row'=32,'col_0'=4,'col_1'=2] {'row'}, dimensions={0} | all-to-all | bytes 262144 | tf_op jit(solution)/shard_map/all_to_all | solution.py:48
  247.4 9.1 %all-to-all-start.13 = ((f32[2,4,512,256]{3,2,1,0:T(8,128)}), f32[2,4,512,256]{3,2,1,0:T(8,128)}, u32[]{:S(2)}, u32[]{:S(2)}) async-start(f32[2,4,512,256]{3,2,1,0:T(8,128)} %broadcast_in_dim.46), calls=%async_computation.13 | async-start | bytes 8388608 | tf_op jit(solution)/shard_map/all_to_all | solution.py:13
  256.6 4.1 %all-to-all-done.13 = f32[2,4,512,256]{3,2,1,0:T(8,128)} async-done(((f32[2,4,512,256]{3,2,1,0:T(8,128)}), f32[2,4,512,256]{3,2,1,0:T(8,128)}, u32[]{:S(2)}, u32[]{:S(2)}) %all-to-all-start.13) | async-done | bytes 4194336 | tf_op jit(solution)/shard_map/all_to_all | solution.py:13
  261.3 4.1 %all-to-all-start.11 = ((f32[32,8,128]{2,1,0:T(8,128)}), f32[32,8,128]{2,1,0:T(8,128)S(1)}, u32[]{:S(2)}, u32[]{:S(2)}) async-start(f32[32,8,128]{2,1,0:T(8,128)} %broadcast_in_dim.44), calls=%async_computation.11 | async-start | bytes 262144 | tf_op jit(solution)/shard_map/all_to_all | solution.py:13
  265.5 4.6 %copy.32 = f32[2,4,512,256]{3,2,0,1:T(8,128)} copy(f32[2,4,512,256]{3,2,1,0:T(8,128)} %all-to-all-done.13) | data formatting | bytes 8388608 | tf_op jit(solution)/shard_map/all_to_all | solution.py:13
  270.1 4.3 %all-to-all-done.11 = f32[32,8,128]{2,1,0:T(8,128)S(1)} async-done(((f32[32,8,128]{2,1,0:T(8,128)}), f32[32,8,128]{2,1,0:T(8,128)S(1)}, u32[]{:S(2)}, u32[]{:S(2)}) %all-to-all-start.11) | async-done | bytes 131104 | tf_op jit(solution)/shard_map/all_to_all | solution.py:13
  274.8 6.7 %fusion.1 = f32[4096,128]{0,1:T(8,128)S(1)} fusion(f32[4096,128]{0,1:T(8,128)S(1)} %copy-done.6, f32[128,256]{1,0:T(8,128)S(1)} %fusion.9, f32[4096,256]{1,0:T(8,128)} %bitcast.94), kind=kOutput, calls=%fused_computation.3 | convolution fusion | flops 1611137024 | bytes 8519680 | tf_op jit(solution)/shard_map/dot_general | solution.py:60
  284.9 13.7 %all_to_all.87 = f32[32,8,128]{2,1,0:T(8,128)S(1)} all-to-all(f32[32,8,128]{2,1,0:T(8,128)S(1)} %bitcast.101), channel_id=1, replica_groups=mesh['row'=32,'col_0'=4,'col_1'=2] {'row'}, dimensions={0} | all-to-all | bytes 262144 | tf_op jit(solution)/shard_map/all_to_all | solution.py:48
  298.6 12.7 %all_to_all.88 = f32[32,8,128]{2,1,0:T(8,128)S(1)} all-to-all(f32[32,8,128]{2,1,0:T(8,128)S(1)} %broadcast_in_dim.47), channel_id=1, replica_groups=mesh['row'=32,'col_0'=4,'col_1'=2] {'row'}, dimensions={0} | all-to-all | bytes 262144 | tf_op jit(solution)/shard_map/all_to_all | solution.py:13
  311.8 7.2 %fusion = f32[4096,128]{0,1:T(8,128)S(1)} fusion(f32[4096,128]{0,1:T(8,128)} %copy-done.7, f32[128,256]{1,0:T(8,128)S(1)} %fusion.7, f32[4096,256]{1,0:T(8,128)} %bitcast.97), kind=kOutput, calls=%fused_computation.1 | convolution fusion | flops 1611137024 | bytes 8519680 | tf_op jit(solution)/shard_map/dot_general | solution.py:60
  (54 shorter events, 40.0 us)
Async XLA Ops:
  45.2 30.6 %all-to-all-start.4 = ((f32[4,512,256]{2,1,0:T(8,128)}), f32[4,512,256]{2,1,0:T(8,128)}, u32[]{:S(2)}, u32[]{:S(2)}) async-start(f32[4,512,256]{2,1,0:T(8,128)} %broadcast_in_dim.39), calls=%async_computation.4 | async-start | bytes 4194304 | tf_op jit(solution)/shard_map/all_to_all | solution.py:13
  55.0 5.8 %copy-start.8 = (f32[4096,128]{1,0:T(8,128)S(1)}, f32[4096,128]{1,0:T(8,128)}, u32[]{:S(2)}) copy-start(f32[4096,128]{1,0:T(8,128)} %param.3) | copy-start | bytes 6291460
  99.9 12.4 %all-to-all-start.5 = ((f32[2,4,512,256]{3,2,1,0:T(8,128)}), f32[2,4,512,256]{3,2,1,0:T(8,128)}, u32[]{:S(2)}, u32[]{:S(2)}) async-start(f32[2,4,512,256]{3,2,1,0:T(8,128)} %broadcast_in_dim.40), calls=%async_computation.5 | async-start | bytes 8388608 | tf_op jit(solution)/shard_map/all_to_all | solution.py:13
  126.2 28.9 %all-to-all-start.8 = ((f32[4,512,256]{2,1,0:T(8,128)}), f32[4,512,256]{2,1,0:T(8,128)}, u32[]{:S(2)}, u32[]{:S(2)}) async-start(f32[4,512,256]{2,1,0:T(8,128)} %broadcast_in_dim.42), calls=%async_computation.8 | async-start | bytes 4194304 | tf_op jit(solution)/shard_map/all_to_all | solution.py:13
  132.7 5.4 %copy-start.3 = (f32[2,4,512,256]{3,2,0,1:T(8,128)S(1)}, f32[2,4,512,256]{3,2,0,1:T(8,128)}, u32[]{:S(2)}) copy-start(f32[2,4,512,256]{3,2,0,1:T(8,128)} %copy.25) | copy-start | bytes 12582916
  132.7 5.4 %copy-start.9 = (f32[4096,128]{0,1:T(8,128)S(1)}, f32[4096,128]{0,1:T(8,128)}, u32[]{:S(2)}) copy-start(f32[4096,128]{0,1:T(8,128)} %copy.27) | copy-start | bytes 6291460
  135.5 7.0 %copy-start = (f32[2,4,512,256]{3,2,0,1:T(8,128)}, f32[2,4,512,256]{3,2,0,1:T(8,128)S(1)}, u32[]{:S(2)}) copy-start(f32[2,4,512,256]{3,2,0,1:T(8,128)S(1)} %copy.28) | copy-start | bytes 12582916
  173.3 13.2 %all-to-all-start.9 = ((f32[2,4,512,256]{3,2,1,0:T(8,128)}), f32[2,4,512,256]{3,2,1,0:T(8,128)}, u32[]{:S(2)}, u32[]{:S(2)}) async-start(f32[2,4,512,256]{3,2,1,0:T(8,128)} %broadcast_in_dim.43), calls=%async_computation.9 | async-start | bytes 8388608 | tf_op jit(solution)/shard_map/all_to_all | solution.py:13
  200.4 28.9 %all-to-all-start.12 = ((f32[4,512,256]{2,1,0:T(8,128)}), f32[4,512,256]{2,1,0:T(8,128)}, u32[]{:S(2)}, u32[]{:S(2)}) async-start(f32[4,512,256]{2,1,0:T(8,128)} %broadcast_in_dim.45), calls=%async_computation.12 | async-start | bytes 4194304 | tf_op jit(solution)/shard_map/all_to_all | solution.py:13
  205.1 2.8 copy-start.10
  205.1 3.8 %copy-start.1 = (f32[2,4,512,256]{3,2,0,1:T(8,128)S(1)}, f32[2,4,512,256]{3,2,0,1:T(8,128)}, u32[]{:S(2)}) copy-start(f32[2,4,512,256]{3,2,0,1:T(8,128)} %copy-done) | copy-start | bytes 12582916
  207.9 5.3 %copy-start.2 = (f32[2,4,512,256]{3,2,0,1:T(8,128)}, f32[2,4,512,256]{3,2,0,1:T(8,128)S(1)}, u32[]{:S(2)}) copy-start(f32[2,4,512,256]{3,2,0,1:T(8,128)S(1)} %copy.30) | copy-start | bytes 12582916
  213.3 1.3 copy-start.5
  247.4 13.2 %all-to-all-start.13 = ((f32[2,4,512,256]{3,2,1,0:T(8,128)}), f32[2,4,512,256]{3,2,1,0:T(8,128)}, u32[]{:S(2)}, u32[]{:S(2)}) async-start(f32[2,4,512,256]{3,2,1,0:T(8,128)} %broadcast_in_dim.46), calls=%async_computation.13 | async-start | bytes 8388608 | tf_op jit(solution)/shard_map/all_to_all | solution.py:13
  261.3 13.0 %all-to-all-start.11 = ((f32[32,8,128]{2,1,0:T(8,128)}), f32[32,8,128]{2,1,0:T(8,128)S(1)}, u32[]{:S(2)}, u32[]{:S(2)}) async-start(f32[32,8,128]{2,1,0:T(8,128)} %broadcast_in_dim.44), calls=%async_computation.11 | async-start | bytes 262144 | tf_op jit(solution)/shard_map/all_to_all | solution.py:13
  265.5 9.3 %copy-start.6 = (f32[4096,128]{0,1:T(8,128)S(1)}, f32[4096,128]{0,1:T(8,128)}, u32[]{:S(2)}) copy-start(f32[4096,128]{0,1:T(8,128)} %copy-done.5) | copy-start | bytes 6291460
  274.7 8.0 %copy-start.4 = (f32[2,4,512,256]{3,2,0,1:T(8,128)S(1)}, f32[2,4,512,256]{3,2,0,1:T(8,128)}, u32[]{:S(2)}) copy-start(f32[2,4,512,256]{3,2,0,1:T(8,128)} %copy.32) | copy-start | bytes 12582916
  281.4 1.3 copy-start.7
where the time goes:
time: 323 us; the launch traced here: 321 us
  blocking collectives  139 us (43%)
  local copies, waits for them, and re-layouts  49.4 us (15%)
  waiting for transfers between devices  48.5 us (15%)
  starting transfers between devices  44.5 us (14%)
  matrix products  38.5 us (12%)
    all_to_all x5, blocking collectives, copy_for_each(): return lax.all_to_all(copies, axis, split_axis=0, concat_axis=0, tiled=True)  77 us
    all_to_all x4, blocking collectives, summed_on_arrival(): lax.all_to_all(tiles, axis, split_axis=0, concat_axis=0, tiled=True)  62.4 us
    all_to_all x7, waiting for transfers between devices, copy_for_each(): return lax.all_to_all(copies, axis, split_axis=0, concat_axis=0, tiled=True)  48.5 us
    all_to_all x7, starting transfers between devices, copy_for_each(): return lax.all_to_all(copies, axis, split_axis=0, concat_axis=0, tiled=True)  44.5 us
    dot_general x8, matrix products, product(): jnp.dot(left, right, precision=lax.Precision.HIGHEST, preferred_element_t...  26.3 us
    broadcast_in_dim x12, local copies, waits for them, and re-layouts, copy_for_each(): copies = jnp.broadcast_to(x, (lax.axis_size(axis), *x.shape))  17.8 us
    all_to_all x5, local copies, waits for them, and re-layouts, copy_for_each(): return lax.all_to_all(copies, axis, split_axis=0, concat_axis=0, tiled=True)  16.8 us
    dot_general x4, matrix products, inner(): lax.dot_general(left, right, (((0,), (0,)), ((), ())), precision=lax.Prec...  12.2 us
  transfers between devices with their start and end apart: 7, of which 7 were waited for; matrix products, arithmetic and copies ran while one was open for 14% of the time, Pallas kernels for 0%

commit v1 on v0

v1 whole, which is shorter than its diff:
```python
import jax
import jax.numpy as jnp
from jax import lax
from jax.experimental import pallas as pl
from jax.experimental.pallas import tpu as pltpu
from jax.sharding import PartitionSpec as P

MESH = pl.DeviceIdType.MESH
F32 = jnp.float32
BF16 = jnp.bfloat16

NX, NY, NZ, NC = 4, 4, 8, 2
PANELS, WB = 4, 256
ROWS, COLS = 4096, 128
OWN = 512
CHIP = NC * OWN
CH = 4
CW = COLS // CH
CM = NX * CW
ZW = CM // NZ
PAIRS = [(0, 1), (0, 2), (0, 3), (1, 2), (1, 3), (2, 3)]
HALF = len(PAIRS) // NC
HA = 2 * WB
HB = HALF * WB - HA
HAY, HAZ = HA // NY, HA // NY // NZ
HBZ, HBY = HB // NZ, HB // NZ // NY
HX = HAZ + HBY


def split(x):
    high = x.astype(BF16)
    return high, (x - high.astype(F32)).astype(BF16)


def dot3(a, b, dims):
    def one(left, right):
        return lax.dot_general(left, right, (dims, ((), ())), preferred_element_type=F32)

    (ah, al), (bh, bl) = a, b
    return one(ah, bh) + (one(al, bh) + one(ah, bl))


NN = ((1,), (0,))
NT = ((1,), (1,))
TN = ((0,), (0,))


def kernel(
    f_hbm, v_hbm, t_hbm, out_hbm,
    fv, ft, vown, vsib, tv, th, tl, vh, vl, wh, wl, fin, qp, yr, ys, zr, zs, xr, qf, sol, ut, uin,
    gp, gc, gs, ayr, ays, azr, bzr, bzs, byr, gx, gxr, gf, gh, gl,
    lsem, ssem, rsem, csem,
):
    row, col = lax.axis_index("row"), lax.axis_index("col")
    y, z, x, c = row // NZ, row % NZ, col // NC, col % NC

    def device(nx=x, ny=y, nz=z, nc=c):
        return (ny * NZ + nz, nx * NC + nc)

    def along(axis, d):
        if axis == "x":
            pos = lax.rem(x + d, NX)
            return pos, device(nx=pos)
        if axis == "y":
            pos = lax.rem(y + d, NY)
            return pos, device(ny=pos)
        if axis == "z":
            pos = lax.rem(z + d, NZ)
            return pos, device(nz=pos)
        pos = lax.rem(c + d, NC)
        return pos, device(nc=pos)

    sizes = {"x": NX, "y": NY, "z": NZ, "c": NC}
    started = []
    counter = [0]

    def exchange(axis, source, target):
        copies = []
        for d in range(1, sizes[axis]):
            pos, peer = along(axis, d)
            copy = pltpu.make_async_remote_copy(
                src_ref=source(pos), dst_ref=target(d), send_sem=ssem.at[counter[0]], recv_sem=rsem.at[counter[0]],
                device_id=peer, device_id_type=MESH,
            )
            counter[0] += 1
            copy.start()
            copies.append(copy)
        started.extend(copies)
        return copies

    def arrive(copies):
        for copy in copies:
            copy.wait_recv()

    loads = [
        pltpu.make_async_copy(f_hbm, fv, lsem.at[0]),
        pltpu.make_async_copy(v_hbm, vown, lsem.at[1]),
        pltpu.make_async_copy(t_hbm, tv, lsem.at[2]),
    ]
    for load in loads:
        load.start()

    barrier = pltpu.get_barrier_semaphore()
    peers = 0
    for axis in ("x", "y", "z", "c"):
        for d in range(1, sizes[axis]):
            pl.semaphore_signal(barrier, inc=1, device_id=along(axis, d)[1], device_id_type=MESH)
            peers += 1

    loads[0].wait()

    @pl.loop(0, ROWS // 128)
    def _(b):
        at = pl.multiple_of(b * 128, 128)
        ft[:, pl.ds(at, 128)] = fv[pl.ds(at, 128), :].T

    pl.semaphore_wait(barrier, peers)

    def chip_rows(pos):
        return pl.ds(pl.multiple_of(pos * CHIP, CHIP), CHIP)

    def part(pos, size):
        return pl.ds(pl.multiple_of(pos * size, size), size)

    def send_in(h):
        rows = pl.ds(h * CW, CW)
        copies = exchange("x", lambda pos: ft.at[rows, chip_rows(pos)], lambda d: fin.at[h, part(x, CW), :])
        fin[h, part(x, CW), :] = ft[rows, chip_rows(x)]
        return copies

    ins = {0: send_in(0)}
    loads[1].wait()
    sib = exchange("c", lambda pos: v_hbm, lambda d: vsib)
    ins[1] = send_in(1)

    loads[2].wait()
    for k in range(PANELS):
        th[k], tl[k] = split(tv[k])

    def prepare(source, where):
        rows = part(where, OWN)

        @pl.loop(0, PANELS)
        def _(k):
            high, low = split(source[k])
            vh[k, rows, :] = high
            vl[k, rows, :] = low
            w = dot3((high, low), (th[k], tl[k]), NN)
            high, low = split(w)
            wh[k, rows, :] = high
            wl[k, rows, :] = low

    prepare(vown, c)
    mine = part(c, OWN)
    for index, (j, k) in enumerate(PAIRS):
        gp[pl.ds(index * WB, WB), :] = dot3((wh[j, mine, :], wl[j, mine, :]), (vh[k, mine, :], vl[k, mine, :]), TN)

    share = HALF * WB
    gcs = exchange("c", lambda pos: gp.at[part(pos, share), :], lambda d: gc)
    arrive(gcs)
    gs[...] = gp[part(c, share), :] + gc[...]
    ay = exchange("y", lambda pos: gs.at[part(pos, HAY), :], lambda d: ayr.at[d - 1])
    bz = exchange("z", lambda pos: gs.at[pl.ds(pl.multiple_of(HA + pos * HBZ, HBZ), HBZ), :], lambda d: bzr.at[d - 1])

    arrive(sib)
    prepare(vsib, 1 - c)

    def project(h):
        high, low = split(fin[h])

        @pl.loop(0, PANELS)
        def _(k):
            qp[h, k] = dot3((high, low), (vh[k], vl[k]), NN)

    def send_yrs(h):
        return exchange("y", lambda pos: qp.at[h, pos], lambda d: yr.at[h, d - 1])

    def sum_yrs(h):
        ys[h] = (qp[h, y] + yr[h, 0]) + (yr[h, 1] + yr[h, 2])

    def send_zrs(h):
        return exchange("z", lambda pos: ys.at[h, part(pos, ZW), :], lambda d: zr.at[h, d - 1])

    def sum_zrs(h):
        total = ys[h, part(z, ZW), :]
        for d in range(NZ - 1):
            total = total + zr[h, d]
        zs[h] = total

    def send_x(h):
        return exchange("x", lambda pos: zs.at[h], lambda d: xr.at[h, d - 1])

    def sum_x(h):
        qf[h, y, part(z, ZW), :] = (zs[h] + xr[h, 0]) + (xr[h, 1] + xr[h, 2])

    def send_zag(h):
        here = qf.at[h, y, part(z, ZW), :]
        return exchange("z", lambda pos: here, lambda d: here)

    def send_yag(h):
        here = qf.at[h, y]
        return exchange("y", lambda pos: here, lambda d: here)

    def pair(j, k):
        return pl.ds(PAIRS.index((j, k)) * WB, WB)

    def solve(h):
        proj = [qf[h, k] for k in range(PANELS)]
        for j in range(PANELS):
            high, low = split(proj[j])
            sol[h, 0, j] = high
            sol[h, 1, j] = low
            for k in range(j + 1, PANELS):
                proj[k] = proj[k] - dot3((high, low), (gh[pair(j, k), :], gl[pair(j, k), :]), NN)
        ut[h] = jnp.zeros((CM, CHIP), F32)

        @pl.loop(0, PANELS)
        def _(k):
            ut[h] += dot3((sol[h, 0, k], sol[h, 1, k]), (wh[k], wl[k]), NT)

    def send_out(h):
        rows = pl.ds(h * CW, CW)
        copies = exchange("x", lambda pos: ut.at[h, part(pos, CW), :], lambda d: uin.at[rows, chip_rows(x)])
        uin[rows, chip_rows(x)] = ut[h, part(x, CW), :]
        return copies

    def pairs_first():
        arrive(ay)
        ays[...] = (gs[part(y, HAY), :] + ayr[0]) + (ayr[1] + ayr[2])
        arrive(bz)
        total = gs[pl.ds(pl.multiple_of(HA + z * HBZ, HBZ), HBZ), :]
        for d in range(NZ - 1):
            total = total + bzr[d]
        bzs[...] = total
        az = exchange("z", lambda pos: ays.at[part(pos, HAZ), :], lambda d: azr.at[d - 1])
        by = exchange("y", lambda pos: bzs.at[part(pos, HBY), :], lambda d: byr.at[d - 1])
        return az, by

    def pairs_second(az, by):
        arrive(az)
        total = ays[part(z, HAZ), :]
        for d in range(NZ - 1):
            total = total + azr[d]
        gx[pl.ds(0, HAZ), :] = total
        arrive(by)
        gx[pl.ds(HAZ, HBY), :] = (bzs[part(y, HBY), :] + byr[0]) + (byr[1] + byr[2])
        return exchange("x", lambda pos: gx, lambda d: gxr.at[d - 1])

    base = c * share
    spot_a = pl.ds(pl.multiple_of(base + y * HAY + z * HAZ, HAZ), HAZ)
    line_a = pl.ds(pl.multiple_of(base + y * HAY, HAY), HAY)
    spot_b = pl.ds(pl.multiple_of(base + HA + z * HBZ + y * HBY, HBY), HBY)
    line_b = pl.ds(pl.multiple_of(base + HA + z * HBZ, HBZ), HBZ)

    def pairs_third(copies):
        arrive(copies)
        total = (gx[...] + gxr[0]) + (gxr[1] + gxr[2])
        gf[spot_a, :] = total[:HAZ]
        gf[spot_b, :] = total[HAZ:]
        az = exchange("z", lambda pos: gf.at[spot_a, :], lambda d: gf.at[spot_a, :])
        by = exchange("y", lambda pos: gf.at[spot_b, :], lambda d: gf.at[spot_b, :])
        return az, by

    def pairs_fourth(az, by):
        arrive(az)
        arrive(by)
        ay = exchange("y", lambda pos: gf.at[line_a, :], lambda d: gf.at[line_a, :])
        bz = exchange("z", lambda pos: gf.at[line_b, :], lambda d: gf.at[line_b, :])
        return ay, bz

    def pairs_fifth(ay, bz):
        arrive(ay)
        arrive(bz)
        return exchange("c", lambda pos: gf.at[part(c, share), :], lambda d: gf.at[part(c, share), :])

    def pairs_last(copies):
        arrive(copies)
        gh[...], gl[...] = split(gf[...])

    yrs, zrs, xs, zag, yag, outs = {}, {}, {}, {}, {}, {}

    def step_in(h):
        arrive(ins[h])
        if h + 2 < CH:
            ins[h + 2] = send_in(h + 2)
        project(h)
        yrs[h] = send_yrs(h)

    def step_y(h):
        arrive(yrs[h])
        sum_yrs(h)
        zrs[h] = send_zrs(h)

    def step_z(h):
        arrive(zrs[h])
        sum_zrs(h)
        xs[h] = send_x(h)

    def step_x(h):
        arrive(xs[h])
        sum_x(h)
        zag[h] = send_zag(h)

    def step_zag(h):
        arrive(zag[h])
        yag[h] = send_yag(h)

    def step_out(h):
        arrive(yag[h])
        solve(h)
        outs[h] = send_out(h)

    step_in(0)
    first = pairs_first()
    step_in(1)
    step_y(0)
    second = pairs_second(*first)
    step_in(2)
    step_z(0)
    third = pairs_third(second)
    step_y(1)
    step_in(3)
    step_x(0)
    step_z(1)
    fourth = pairs_fourth(*third)
    step_y(2)
    step_zag(0)
    step_x(1)
    step_z(2)
    step_y(3)
    fifth = pairs_fifth(*fourth)
    step_zag(1)
    step_x(2)
    pairs_last(fifth)
    step_out(0)
    step_z(3)
    step_zag(2)
    step_out(1)
    step_x(3)
    step_zag(3)
    step_out(2)
    step_out(3)

    for h in range(CH):
        arrive(outs[h])

    @pl.loop(0, ROWS // 128)
    def _(b):
        at = pl.multiple_of(b * 128, 128)
        fv[pl.ds(at, 128), :] = fv[pl.ds(at, 128), :] - uin[:, pl.ds(at, 128)].T

    for copy in started:
        copy.wait_send()
    store = pltpu.make_async_copy(fv, out_hbm, csem)
    store.start()
    store.wait()


COPIES = NC - 1 + CH * (4 * (NX - 1) - 1 * (NX - 1) + 2 * (NY - 1) + 2 * (NZ - 1)) + 2 * (NC - 1) + 4 * (NY - 1) + 4 * (NZ - 1) + (NX - 1)


def body(eigvecs, reflectors, factors):
    def vm(shape, dtype=F32):
        return pltpu.VMEM(shape, dtype)

    scratch = [
        vm((ROWS, COLS)), vm((COLS, ROWS)), vm((PANELS, OWN, WB)), vm((PANELS, OWN, WB)), vm((PANELS, WB, WB)),
        vm((PANELS, WB, WB), BF16), vm((PANELS, WB, WB), BF16),
        vm((PANELS, CHIP, WB), BF16), vm((PANELS, CHIP, WB), BF16), vm((PANELS, CHIP, WB), BF16), vm((PANELS, CHIP, WB), BF16),
        vm((CH, CM, CHIP)), vm((CH, PANELS, CM, WB)), vm((CH, NY - 1, CM, WB)), vm((CH, CM, WB)),
        vm((CH, NZ - 1, ZW, WB)), vm((CH, ZW, WB)), vm((CH, NX - 1, ZW, WB)), vm((CH, PANELS, CM, WB)),
        vm((CH, 2, PANELS, CM, WB), BF16), vm((CH, CM, CHIP)), vm((COLS, ROWS)),
        vm((len(PAIRS) * WB, WB)), vm((HALF * WB, WB)), vm((HALF * WB, WB)),
        vm((NY - 1, HAY, WB)), vm((HAY, WB)), vm((NZ - 1, HAZ, WB)), vm((NZ - 1, HBZ, WB)), vm((HBZ, WB)), vm((NY - 1, HBY, WB)),
        vm((HX, WB)), vm((NX - 1, HX, WB)), vm((len(PAIRS) * WB, WB)), vm((len(PAIRS) * WB, WB), BF16), vm((len(PAIRS) * WB, WB), BF16),
        pltpu.SemaphoreType.DMA((3,)), pltpu.SemaphoreType.DMA((COPIES,)), pltpu.SemaphoreType.DMA((COPIES,)), pltpu.SemaphoreType.DMA,
    ]
    return pl.pallas_call(
        kernel,
        out_shape=jax.ShapeDtypeStruct((ROWS, COLS), F32),
        in_specs=[pl.BlockSpec(memory_space=pl.ANY)] * 3,
        out_specs=pl.BlockSpec(memory_space=pl.ANY),
        scratch_shapes=scratch,
        compiler_params=pltpu.CompilerParams(collective_id=0, has_side_effects=True, vmem_limit_bytes=63 * 2**20),
        name="back_transform",
    )(eigvecs, reflectors, factors)


def solution(mesh):
    in_specs = (P("row", "col"), P(None, ("row", "col"), None), P())
    return jax.shard_map(body, mesh=mesh, in_specs=in_specs, out_specs=P("row", "col"), check_vma=False)
```

time: 323 us -> 107 us (0.33)
  blocking collectives: 139 us -> 0 us
  Pallas kernels: 0 us -> 103 us
  waiting for transfers between devices: 48.5 us -> 0 us
  local copies, waits for them, and re-layouts: 49.4 us -> 3.05 us
  starting transfers between devices: 44.5 us -> 0 us
  matrix products: 38.5 us -> 0 us
    all_to_all x9 -> x0, blocking collectives: 139 us -> none  [the longest x5 77 us: copy_for_each(): return lax.all_to_all(copies, axis, split_axis=0, concat_axis=0, tiled=True)]
    pallas_call x0 -> x1, Pallas kernels: none -> 103 us  [body(): pl.pallas_call(kernel, out_shape=jax.ShapeDtypeStruct((ROWS, COLS), F32),...]
    all_to_all x7 -> x0, waiting for transfers between devices: 48.5 us -> none  [copy_for_each(): return lax.all_to_all(copies, axis, split_axis=0, concat_axis=0, tiled=True)]
    all_to_all x7 -> x0, starting transfers between devices: 44.5 us -> none  [copy_for_each(): return lax.all_to_all(copies, axis, split_axis=0, concat_axis=0, tiled=True)]
    dot_general x12 -> x0, matrix products: 38.5 us -> none  [the longest x8 26.3 us: product(): jnp.dot(left, right, precision=lax.Precision.HIGHEST, preferred_element_t...]
    broadcast_in_dim x12 -> x0, local copies, waits for them, and re-layouts: 17.8 us -> none  [copy_for_each(): copies = jnp.broadcast_to(x, (lax.axis_size(axis), *x.shape))]
    all_to_all x5 -> x0, local copies, waits for them, and re-layouts: 16.8 us -> none  [copy_for_each(): return lax.all_to_all(copies, axis, split_axis=0, concat_axis=0, tiled=True)]
    dot_general x4 -> x0, local copies, waits for them, and re-layouts: 6.08 us -> none  [inner(): lax.dot_general(left, right, (((0,), (0,)), ((), ())), precision=lax.Prec...]
  transfers between devices with their start and end apart: 7 -> 0, of which waited for: 7 -> 0; matrix products, arithmetic and copies ran while one was open for 14% -> 0% of each run, Pallas kernels for 0% -> 0%
where the time goes in v1:
time: 107 us; the launch traced here: 106 us
  Pallas kernels  103 us (96%)
  local copies, waits for them, and re-layouts  3.05 us (3%)
    pallas_call x1, Pallas kernels, body(): pl.pallas_call(kernel, out_shape=jax.ShapeDtypeStruct((ROWS, COLS), F32),...  103 us
    unnamed x1, local copies, waits for them, and re-layouts  3.05 us

profile of v1, /device:TPU:1, one launch (start us, length us, event | category | flops | bytes accessed | tf_op | source)
XLA Modules:
  0.0 105.7 jit_solution(1783376225002414835)
XLA Ops:
  0.0 102.7 %back_transform.1 = f32[4096,128]{1,0:T(8,128)} custom-call(f32[4096,128]{1,0:T(8,128)} %f_hbm.1, f32[4,512,256]{2,1,0:T(8,128)} %v_hbm.1, f32[4,256,256]{2,1,0:T(8,128)} %t_hbm.1), custom_call_target="tpu_custom_call" | custom-call | tf_op jit(solution)/shard_map/back_transform/pallas_call | solution.py:378
  102.7 3.0 %copy.5 = f32[4096,128]{1,0:T(8,128)} copy(f32[4096,128]{1,0:T(8,128)} %back_transform.1) | data formatting | bytes 4194304

commit v2 on v0

v2 whole, which is shorter than its diff:
```python
import jax
import jax.numpy as jnp
from jax import lax
from jax.experimental import pallas as pl
from jax.experimental.pallas import tpu as pltpu
from jax.sharding import PartitionSpec as P

MESH = pl.DeviceIdType.MESH
F32 = jnp.float32
BF16 = jnp.bfloat16

SIZES = {"x": 4, "y": 4, "z": 8, "c": 2}
NX, NY, NZ, NC = SIZES.values()
PANELS, WB = 4, 256
ROWS, COLS = 4096, 128
OWN = 512
CHIP = NC * OWN
WIDE = PANELS * WB
CH = 8
CW = COLS // CH
CM = NX * CW
PAIRS = [(0, 1), (0, 2), (0, 3), (1, 2), (1, 3), (2, 3)]
SHARE = len(PAIRS) // NC * WB
HA = 2 * WB
HB = SHARE - HA
AM = HA // NY
BZ, BY = HB // NZ, HB // NZ // NY
A = CH
ORDER = [
    ("gc",), ("next", 1), ("next", 2), ("next", 3), ("next", 4), ("next", 5), ("sib",), ("in", 0), ("in", 1), ("r1", A),
    ("r1", 0), ("b1",), ("in", 3), ("b2",), ("in", 4), ("r1", 1), ("r2", A), ("b3",), ("next", 6), ("x", A), ("in", 2), ("r1", 3),
    ("r1", 4), ("r2", 1), ("b4",), ("a1", A), ("next", 7), ("in", 6), ("r1", 2), ("r2", 3), ("in", 5), ("x", 1), ("r2", 4),
    ("a2", A), ("in", 7), ("x", 4), ("x", 3), ("r1", 6), ("r2", 2), ("r1", 5), ("r2", 0), ("a1", 1), ("pairs",), ("a1", 4),
    ("x", 2), ("r1", 7), ("x", 0), ("fold", 2), ("fold", 1), ("a1", 3), ("fold", 0), ("r2", 6), ("r2", 5), ("out", 1), ("x", 6),
    ("r2", 7), ("a1", 2), ("x", 5), ("out", 4), ("a1", 0), ("out", 3), ("a1", 6), ("x", 7), ("out", 2), ("a1", 5), ("out", 0),
    ("a1", 7), ("out", 6), ("out", 5), ("out", 7),
]


def split(x):
    high = x.astype(BF16)
    return high, (x - high.astype(F32)).astype(BF16)


def dot3(a, b, dims=((1,), (0,))):
    def one(left, right):
        return lax.dot_general(left, right, (dims, ((), ())), preferred_element_type=F32)

    (ah, al), (bh, bl) = a, b
    return one(ah, bh) + (one(al, bh) + one(ah, bl))


def part(pos, size):
    return pl.ds(pl.multiple_of(pos * size, size), size)


def added(first, arrived):
    total = first
    for d in range(arrived.shape[0]):
        total = total + arrived[d]
    return total


def kernel(
    f_hbm, v_hbm, t_hbm, out_hbm,
    fv, ft, vown, vsib, tv, th, tl, vh, vl, wh, wl, fin, qp, yr, ys, zr, zs, xr, qf, ut, uin,
    gp, gc, aq, ayr, ays, azr, azs, axr, aqx, gb, bzr, bzs, byr, bys, bxr, gf, gh, gl,
    lsem, ssem, rsem, csem,
):
    row, col = lax.axis_index("row"), lax.axis_index("col")
    at = {"x": col // NC, "y": row // NZ, "z": row % NZ, "c": col % NC}
    x, y, z, c = at.values()
    started = []

    def along(axis, d):
        pos = lax.rem(at[axis] + d, SIZES[axis])
        to = {**at, axis: pos}
        return pos, (to["y"] * NZ + to["z"], to["x"] * NC + to["c"])

    def exchange(axis, source, target):
        sent = []
        for d in range(1, SIZES[axis]):
            pos, peer = along(axis, d)
            index = len(started)
            copy = pltpu.make_async_remote_copy(
                src_ref=source(pos), dst_ref=target(d), send_sem=ssem.at[index], recv_sem=rsem.at[index],
                device_id=peer, device_id_type=MESH,
            )
            copy.start()
            sent.append(copy)
            started.append(copy)
        return sent

    def arrive(sent):
        for copy in sent:
            copy.wait_recv()

    loads = [
        pltpu.make_async_copy(f_hbm, fv, lsem.at[0]),
        pltpu.make_async_copy(t_hbm, tv, lsem.at[1]),
        pltpu.make_async_copy(v_hbm, vown, lsem.at[2]),
    ]
    for load in loads:
        load.start()

    barrier = pltpu.get_barrier_semaphore()
    peers = 0
    for axis, size in SIZES.items():
        for d in range(1, size):
            pl.semaphore_signal(barrier, inc=1, device_id=along(axis, d)[1], device_id_type=MESH)
            peers += 1

    loads[0].wait()

    @pl.loop(0, ROWS // 512)
    def _(b):
        for u in range(4):
            rows = pl.ds(pl.multiple_of(b * 512 + u * 128, 128), 128)
            ft[:, rows] = fv[rows, :].T

    loads[1].wait()
    for k in range(PANELS):
        th[k], tl[k] = split(tv[k].T)
    loads[2].wait()

    def prepare(source, where):
        rows = part(where, OWN)

        @pl.loop(0, PANELS)
        def _(k):
            lanes = part(k, WB)
            v = split(source[k])
            vh[rows, lanes], vl[rows, lanes] = v
            wh[lanes, rows], wl[lanes, rows] = split(dot3((th[k], tl[k]), v, ((1,), (1,))))

    prepare(vown, c)
    mine = part(c, OWN)
    for index, (j, k) in enumerate(PAIRS):
        jl, kl = pl.ds(j * WB, WB), pl.ds(k * WB, WB)
        gp[pl.ds(index * WB, WB), :] = dot3((wh[jl, mine], wl[jl, mine]), (vh[mine, kl], vl[mine, kl]))

    pl.semaphore_wait(barrier, peers)

    copies = {}

    def send_in(h):
        rows = pl.ds(h * CW, CW)
        here = part(x, CW)
        copies["in", h] = exchange("x", lambda pos: ft.at[rows, part(pos, CHIP)], lambda d: fin.at[h, here, :])
        fin[h, here, :] = ft[rows, part(x, CHIP)]

    send_in(0)
    copies["gc"] = exchange("c", lambda pos: gp.at[part(pos, SHARE), :], lambda d: gc)
    copies["sib"] = exchange("c", lambda pos: v_hbm, lambda d: vsib)

    def prepare_sibling():
        arrive(copies["sib"])
        prepare(vsib, 1 - c)

    def stage_in(h):
        arrive(copies["in", h])
        total = dot3(split(fin[h]), (vh[...], vl[...]))
        for k in range(PANELS):
            qp[h, k] = total[:, k * WB : (k + 1) * WB]
        copies["r1", h] = exchange("y", lambda pos: qp.at[h, pos], lambda d: yr.at[h, d - 1])

    def stage_r1(h):
        arrive(copies["r1", h])
        ys[h] = added(qp[h, y], yr.at[h])
        copies["r2", h] = exchange("z", lambda pos: ys.at[h, part(pos, CM // NZ), :], lambda d: zr.at[h, d - 1])

    def stage_r2(h):
        arrive(copies["r2", h])
        zs[h] = added(ys[h, part(z, CM // NZ), :], zr.at[h])
        copies["x", h] = exchange("x", lambda pos: zs.at[h], lambda d: xr.at[h, d - 1])

    def stage_x(h):
        arrive(copies["x", h])
        rows = part(z, CM // NZ)
        qf[h, y, rows, :] = added(zs[h], xr.at[h])
        here = qf.at[h, y, rows, :]
        copies["a1", h] = exchange("z", lambda pos: here, lambda d: here)

    def stage_a1(h):
        arrive(copies["a1", h])
        here = qf.at[h, y]
        copies["a2", h] = exchange("y", lambda pos: here, lambda d: here)

    def stage_out(h):
        arrive(copies["a2", h])
        total = jnp.concatenate([qf[h, k] for k in range(PANELS)], axis=1)
        ut[h] = dot3(split(total), (wh[...], wl[...]))
        rows = pl.ds(h * CW, CW)
        here = part(x, CHIP)
        copies["out", h] = exchange("x", lambda pos: ut.at[h, part(pos, CW), :], lambda d: uin.at[rows, here])
        uin[rows, here] = ut[h, part(x, CW), :]

    def stage_gc():
        arrive(copies["gc"])
        for p in range(NY):
            aq[p] = gp[pl.ds(pl.multiple_of(c * SHARE + p * AM, AM), AM), :] + gc[pl.ds(p * AM, AM), :]
        gb[...] = gp[pl.ds(pl.multiple_of(c * SHARE + HA, HB), HB), :] + gc[pl.ds(HA, HB), :]
        copies["r1", A] = exchange("y", lambda pos: aq.at[pos], lambda d: ayr.at[d - 1])
        copies["b1"] = exchange("z", lambda pos: gb.at[part(pos, BZ), :], lambda d: bzr.at[d - 1])

    def unit(pos):
        return pl.ds(pl.multiple_of(pos // 2 * 8, 8), 8), pl.ds(pl.multiple_of(pos % 2 * 128, 128), 128)

    def pairs_r1():
        arrive(copies["r1", A])
        ays[...] = added(aq[y], ayr)
        copies["r2", A] = exchange("z", lambda pos: ays.at[part(pos, AM // NZ), :], lambda d: azr.at[d - 1])

    def pairs_r2():
        arrive(copies["r2", A])
        azs[...] = added(ays[part(z, AM // NZ), :], azr)
        copies["x", A] = exchange("x", lambda pos: azs.at[*unit(pos)], lambda d: axr.at[d - 1])

    def pairs_x():
        arrive(copies["x", A])
        aqx[x, y, part(z, 8), :] = added(azs[*unit(x)], axr)
        here = aqx.at[x, y, part(z, 8), :]
        copies["a1", A] = exchange("z", lambda pos: here, lambda d: here)

    def pairs_a1():
        arrive(copies["a1", A])
        here = aqx.at[x, y]
        copies["a2", A] = exchange("y", lambda pos: here, lambda d: here)

    def pairs_a2():
        arrive(copies["a2", A])
        here = aqx.at[x]
        copies["a3", A] = exchange("x", lambda pos: here, lambda d: here)

    spot = pl.ds(pl.multiple_of(c * SHARE + HA + z * BZ + y * BY, BY), BY)
    line = pl.ds(pl.multiple_of(c * SHARE + HA + z * BZ, BZ), BZ)

    def stage_b1():
        arrive(copies["b1"])
        bzs[...] = added(gb[part(z, BZ), :], bzr)
        copies["b2"] = exchange("y", lambda pos: bzs.at[part(pos, BY), :], lambda d: byr.at[d - 1])

    def stage_b2():
        arrive(copies["b2"])
        bys[...] = added(bzs[part(y, BY), :], byr)
        copies["b3"] = exchange("x", lambda pos: bys, lambda d: bxr.at[d - 1])

    def stage_b3():
        arrive(copies["b3"])
        gf[spot, :] = added(bys[...], bxr)
        here = gf.at[spot, :]
        copies["b4"] = exchange("y", lambda pos: here, lambda d: here)

    def stage_b4():
        arrive(copies["b4"])
        here = gf.at[line, :]
        copies["b5"] = exchange("z", lambda pos: here, lambda d: here)

    def stage_pairs():
        arrive(copies["a3", A])
        for p in range(NY):
            rows = pl.ds(pl.multiple_of(c * SHARE + p * AM, AM), AM)
            for lane in range(2):
                halves = jnp.stack([aqx[2 * half + lane, p].reshape(NZ, 8, 128) for half in range(2)], 1)
                gf[rows, pl.ds(lane * 128, 128)] = halves.reshape(AM, 128)
        arrive(copies["b5"])
        here = gf.at[part(c, SHARE), :]
        copies["gs"] = exchange("c", lambda pos: here, lambda d: here)

    def fold(j):
        if j == PANELS - 2:
            arrive(copies["gs"])
            gh[...], gl[...] = split(gf[...])
        jl = pl.ds(j * WB, WB)
        total = wh[jl, :].astype(F32) + wl[jl, :].astype(F32)
        for k in range(j + 1, PANELS):
            kl = pl.ds(k * WB, WB)
            pair = pl.ds(PAIRS.index((j, k)) * WB, WB)
            total = total - dot3((gh[pair, :], gl[pair, :]), (wh[kl, :], wl[kl, :]))
        wh[jl, :], wl[jl, :] = split(total)

    stages = {
        "next": send_in, "sib": prepare_sibling, "in": stage_in, "r1": stage_r1, "r2": stage_r2, "x": stage_x,
        "a1": stage_a1, "out": stage_out, "gc": stage_gc, "b1": stage_b1, "b2": stage_b2, "b3": stage_b3, "b4": stage_b4,
        "pairs": stage_pairs, "fold": fold,
    }
    pair_stages = {"r1": pairs_r1, "r2": pairs_r2, "x": pairs_x, "a1": pairs_a1, "a2": pairs_a2}
    for name, *which in ORDER:
        with jax.named_scope("_".join(map(str, [name, *which]))):
            if which == [A]:
                pair_stages[name]()
            else:
                stages[name](*which)

    stores = []

    def finish(pos):
        @pl.loop(0, CHIP // 512)
        def _(b):
            for u in range(4):
                rows = pl.ds(pl.multiple_of(pos * CHIP + b * 512 + u * 128, 128), 128)
                fv[rows, :] = fv[rows, :] - uin[:, rows].T

        store = pltpu.make_async_copy(fv.at[part(pos, CHIP), :], out_hbm.at[part(pos, CHIP), :], csem.at[len(stores)])
        store.start()
        stores.append(store)

    finish(x)
    for d in (1, 3, 2):
        for h in range(CH):
            copies["out", h][d - 1].wait_recv()
        finish(lax.rem(x + NX - d, NX))
    for copy in started:
        copy.wait_send()
    for store in stores:
        store.wait()


COPIES = 2 * (NC - 1) + (NC - 1) + (CH + 1) * (4 * (NX - 1) + 2 * (NY - 1) + 2 * (NZ - 1)) + 2 * (NZ - 1) + 3 * (NX - 1)


def body(eigvecs, reflectors, factors):
    def vm(*shape, dtype=F32):
        return pltpu.VMEM(shape, dtype)

    def half(*shape):
        return [vm(*shape, dtype=BF16)] * 2

    zrows, pairs = CM // NZ, len(PAIRS) * WB
    scratch = [
        vm(ROWS, COLS), vm(COLS, ROWS), vm(PANELS, OWN, WB), vm(PANELS, OWN, WB), vm(PANELS, WB, WB),
        *half(PANELS, WB, WB), *half(CHIP, WIDE), *half(WIDE, CHIP),
        vm(CH, CM, CHIP), vm(CH, PANELS, CM, WB), vm(CH, NY - 1, CM, WB), vm(CH, CM, WB), vm(CH, NZ - 1, zrows, WB),
        vm(CH, zrows, WB), vm(CH, NX - 1, zrows, WB), vm(CH, PANELS, CM, WB), vm(CH, CM, CHIP), vm(COLS, ROWS),
        vm(pairs, WB), vm(SHARE, WB), vm(NY, AM, WB), vm(NY - 1, AM, WB), vm(AM, WB), vm(NZ - 1, AM // NZ, WB),
        vm(AM // NZ, WB), vm(NX - 1, 8, 128), vm(NX, NY, NZ * 8, 128),
        vm(HB, WB), vm(NZ - 1, BZ, WB), vm(BZ, WB), vm(NY - 1, BY, WB), vm(BY, WB), vm(NX - 1, BY, WB),
        vm(pairs, WB), *half(pairs, WB),
        pltpu.SemaphoreType.DMA((3,)), pltpu.SemaphoreType.DMA((COPIES,)), pltpu.SemaphoreType.DMA((COPIES,)),
        pltpu.SemaphoreType.DMA((NX,)),
    ]
    return pl.pallas_call(
        kernel,
        out_shape=jax.ShapeDtypeStruct((ROWS, COLS), F32),
        in_specs=[pl.BlockSpec(memory_space=pl.ANY)] * 3,
        out_specs=pl.BlockSpec(memory_space=pl.ANY),
        scratch_shapes=scratch,
        compiler_params=pltpu.CompilerParams(collective_id=0, has_side_effects=True, vmem_limit_bytes=63 * 2**20),
        name="back_transform",
    )(eigvecs, reflectors, factors)


def solution(mesh):
    in_specs = (P("row", "col"), P(None, ("row", "col"), None), P())
    return jax.shard_map(body, mesh=mesh, in_specs=in_specs, out_specs=P("row", "col"), check_vma=False)
```

time: 323 us -> 94.1 us (0.29)
  blocking collectives: 139 us -> 0 us
  Pallas kernels: 0 us -> 91 us
  waiting for transfers between devices: 48.5 us -> 0 us
  local copies, waits for them, and re-layouts: 49.4 us -> 3.05 us
  starting transfers between devices: 44.5 us -> 0 us
  matrix products: 38.5 us -> 0 us
    all_to_all x9 -> x0, blocking collectives: 139 us -> none  [the longest x5 77 us: copy_for_each(): return lax.all_to_all(copies, axis, split_axis=0, concat_axis=0, tiled=True)]
    pallas_call x0 -> x1, Pallas kernels: none -> 91 us  [body(): pl.pallas_call(kernel, out_shape=jax.ShapeDtypeStruct((ROWS, COLS), F32),...]
    all_to_all x7 -> x0, waiting for transfers between devices: 48.5 us -> none  [copy_for_each(): return lax.all_to_all(copies, axis, split_axis=0, concat_axis=0, tiled=True)]
    all_to_all x7 -> x0, starting transfers between devices: 44.5 us -> none  [copy_for_each(): return lax.all_to_all(copies, axis, split_axis=0, concat_axis=0, tiled=True)]
    dot_general x12 -> x0, matrix products: 38.5 us -> none  [the longest x8 26.3 us: product(): jnp.dot(left, right, precision=lax.Precision.HIGHEST, preferred_element_t...]
    broadcast_in_dim x12 -> x0, local copies, waits for them, and re-layouts: 17.8 us -> none  [copy_for_each(): copies = jnp.broadcast_to(x, (lax.axis_size(axis), *x.shape))]
    all_to_all x5 -> x0, local copies, waits for them, and re-layouts: 16.8 us -> none  [copy_for_each(): return lax.all_to_all(copies, axis, split_axis=0, concat_axis=0, tiled=True)]
    dot_general x4 -> x0, local copies, waits for them, and re-layouts: 6.08 us -> none  [inner(): lax.dot_general(left, right, (((0,), (0,)), ((), ())), precision=lax.Prec...]
  transfers between devices with their start and end apart: 7 -> 0, of which waited for: 7 -> 0; matrix products, arithmetic and copies ran while one was open for 14% -> 0% of each run, Pallas kernels for 0% -> 0%
where the time goes in v2:
time: 94.1 us; the launch traced here: 94 us
  Pallas kernels  91 us (97%)
  local copies, waits for them, and re-layouts  3.05 us (3%)
    pallas_call x1, Pallas kernels, body(): pl.pallas_call(kernel, out_shape=jax.ShapeDtypeStruct((ROWS, COLS), F32),...  91 us
    unnamed x1, local copies, waits for them, and re-layouts  3.05 us

profile of v2, /device:TPU:1, one launch (start us, length us, event | category | flops | bytes accessed | tf_op | source)
XLA Modules:
  0.0 94.0 jit_solution(4281679068672499373)
XLA Ops:
  0.0 91.0 %back_transform.1 = f32[4096,128]{1,0:T(8,128)} custom-call(f32[4096,128]{1,0:T(8,128)} %f_hbm.1, f32[4,512,256]{2,1,0:T(8,128)} %v_hbm.1, f32[4,256,256]{2,1,0:T(8,128)} %t_hbm.1), custom_call_target="tpu_custom_call" | custom-call | tf_op jit(solution)/shard_map/back_transform/pallas_call | solution.py:342
  91.0 3.0 %copy.5 = f32[4096,128]{1,0:T(8,128)} copy(f32[4096,128]{1,0:T(8,128)} %back_transform.1) | data formatting | bytes 4194304

commit v3 on v2

v3 whole, which is shorter than its diff:
```python
import jax
import jax.numpy as jnp
from jax import lax
from jax.experimental import pallas as pl
from jax.experimental.pallas import tpu as pltpu
from jax.sharding import PartitionSpec as P

MESH = pl.DeviceIdType.MESH
F32 = jnp.float32
BF16 = jnp.bfloat16

SIZES = {"x": 4, "y": 4, "z": 8, "c": 2}
NX, NY, NZ, NC = SIZES.values()
PANELS, WB = 4, 256
ROWS, COLS = 4096, 128
OWN = 512
CHIP = NC * OWN
WIDE = PANELS * WB
CH = 8
CW = COLS // CH
CM = NX * CW
PAIRS = [(0, 1), (0, 2), (0, 3), (1, 2), (1, 3), (2, 3)]
SHARE = len(PAIRS) // NC * WB
HA = 2 * WB
HB = SHARE - HA
AM = HA // NY
BZ, BY = HB // NZ, HB // NZ // NY
A = CH
ORDER = [
    ("next", 1), ("next", 2), ("next", 3), ("next", 4), ("gc",), ("sib",), ("in", 0), ("in", 1), ("r1", A), ("in", 2), ("b1",),
    ("r1", 0), ("in", 3), ("next", 5), ("r1", 1), ("in", 4), ("r2", A), ("b2",), ("r1", 2), ("r2", 0), ("next", 6), ("next", 7),
    ("x", A), ("b3",), ("r1", 3), ("in", 5), ("x", 0), ("r2", 1), ("r1", 4), ("a1", A), ("r2", 2), ("b4",), ("in", 6), ("in", 7),
    ("r2", 3), ("x", 1), ("a1", 0), ("a2", A), ("r1", 5), ("r1", 6), ("x", 2), ("r2", 4), ("b5",), ("r1", 7), ("x", 3), ("a1", 1),
    ("fold", 2), ("r2", 5), ("pairs",), ("r2", 6), ("x", 4), ("fold", 1), ("x", 5), ("a1", 2), ("fold", 0), ("out", 0), ("r2", 7),
    ("x", 6), ("a1", 3), ("out", 1), ("a1", 4), ("out", 2), ("a1", 6), ("x", 7), ("a1", 5), ("out", 3), ("out", 4), ("a1", 7),
    ("out", 6), ("out", 5), ("out", 7),
]


def split(x):
    high = x.astype(BF16)
    return high, (x - high.astype(F32)).astype(BF16)


def dot3(a, b, dims=((1,), (0,))):
    def one(left, right):
        return lax.dot_general(left, right, (dims, ((), ())), preferred_element_type=F32)

    (ah, al), (bh, bl) = a, b
    rows = ah.shape[0]
    both = one(jnp.concatenate([ah, al], axis=0), bh)
    return both[:rows] + (both[rows:] + one(ah, bl))


def part(pos, size):
    return pl.ds(pl.multiple_of(pos * size, size), size)


def added(first, arrived):
    total = first
    for d in range(arrived.shape[0]):
        total = total + arrived[d]
    return total


def kernel(
    f_hbm, v_hbm, t_hbm, out_hbm,
    fv, ft, vown, vsib, tv, th, tl, vh, vl, wh, wl, fin, qp, yr, ys, zr, zs, xr, qf, ut, uin,
    gp, gc, aq, ayr, ays, azr, azs, axr, aqx, gb, bzr, bzs, byr, bys, bxr, gf,
    lsem, ssem, rsem, csem,
):
    row, col = lax.axis_index("row"), lax.axis_index("col")
    at = {"x": col // NC, "y": row // NZ, "z": row % NZ, "c": col % NC}
    x, y, z, c = at.values()

    def along(axis, d):
        pos = lax.rem(at[axis] + d, SIZES[axis])
        to = {**at, axis: pos}
        return pos, (to["y"] * NZ + to["z"], to["x"] * NC + to["c"])

    sends = {}
    arrivals = [0]

    def exchange(axis, source, target, whole, kind=None, recv=None):
        slot = sends.setdefault(kind or ("only", len(sends)), (len(sends), whole))[0]
        if recv is None:
            recv = [arrivals[0]] * SIZES[axis]
            arrivals[0] += 1
        for d in range(1, SIZES[axis]):
            pos, peer = along(axis, d)
            pltpu.make_async_remote_copy(
                src_ref=source(pos), dst_ref=target(d), send_sem=ssem.at[slot], recv_sem=rsem.at[recv[d]],
                device_id=peer, device_id_type=MESH,
            ).start()
        return recv[1], whole

    def arrive(sent):
        pltpu.make_async_copy(sent[1], sent[1], rsem.at[sent[0]]).wait()

    loads = [
        pltpu.make_async_copy(t_hbm, tv, lsem.at[1]),
        pltpu.make_async_copy(v_hbm, vown, lsem.at[2]),
        pltpu.make_async_copy(f_hbm, fv, lsem.at[0]),
    ]
    for load in loads:
        load.start()

    barrier = pltpu.get_barrier_semaphore()
    peers = 0
    for axis, size in SIZES.items():
        for d in range(1, size):
            pl.semaphore_signal(barrier, inc=1, device_id=along(axis, d)[1], device_id_type=MESH)
            peers += 1

    loads[0].wait()
    for k in range(PANELS):
        th[k], tl[k] = split(tv[k].T)
    loads[1].wait()

    def prepare(source, where):
        rows = part(where, OWN)

        @pl.loop(0, PANELS)
        def _(k):
            lanes = part(k, WB)
            v = split(source[k])
            vh[rows, lanes], vl[rows, lanes] = v
            wh[lanes, rows], wl[lanes, rows] = split(dot3((th[k], tl[k]), v, ((1,), (1,))))

    prepare(vown, c)
    mine = part(c, OWN)
    for index, (j, k) in enumerate(PAIRS):
        jl, kl = pl.ds(j * WB, WB), pl.ds(k * WB, WB)
        gp[pl.ds(index * WB, WB), :] = dot3((wh[jl, mine], wl[jl, mine]), (vh[mine, kl], vl[mine, kl]))

    pl.semaphore_wait(barrier, peers)

    copies = {}
    back = [None, 0, 1, 2]
    arrivals[0] = NX - 1
    copies["gc"] = exchange("c", lambda pos: gp.at[part(pos, SHARE), :], lambda d: gc, gc)
    copies["sib"] = exchange("c", lambda pos: v_hbm, lambda d: vsib, vsib)

    loads[2].wait()

    @pl.loop(0, ROWS // 512)
    def _(b):
        for u in range(4):
            rows = pl.ds(pl.multiple_of(b * 512 + u * 128, 128), 128)
            ft[:, rows] = fv[rows, :].T


    def send_in(h):
        rows = pl.ds(h * CW, CW)
        here = part(x, CW)
        copies["in", h] = exchange("x", lambda pos: ft.at[rows, part(pos, CHIP)], lambda d: fin.at[h, here, :], fin.at[h, pl.ds(0, CM - CW), :], "in")
        fin[h, here, :] = ft[rows, part(x, CHIP)]

    send_in(0)

    def prepare_sibling():
        arrive(copies["sib"])
        prepare(vsib, 1 - c)

    def stage_in(h):
        arrive(copies["in", h])
        total = dot3(split(fin[h]), (vh[...], vl[...]))
        for k in range(PANELS):
            qp[h, k] = total[:, k * WB : (k + 1) * WB]
        copies["r1", h] = exchange("y", lambda pos: qp.at[h, pos], lambda d: yr.at[h, d - 1], yr.at[h], "r1")

    def stage_r1(h):
        arrive(copies["r1", h])
        ys[h] = added(qp[h, y], yr.at[h])
        copies["r2", h] = exchange("z", lambda pos: ys.at[h, part(pos, CM // NZ), :], lambda d: zr.at[h, d - 1], zr.at[h], "r2")

    def stage_r2(h):
        arrive(copies["r2", h])
        zs[h] = added(ys[h, part(z, CM // NZ), :], zr.at[h])
        copies["x", h] = exchange("x", lambda pos: zs.at[h], lambda d: xr.at[h, d - 1], xr.at[h], "x")

    def stage_x(h):
        arrive(copies["x", h])
        rows = part(z, CM // NZ)
        qf[h, y, rows, :] = added(zs[h], xr.at[h])
        here = qf.at[h, y, rows, :]
        copies["a1", h] = exchange("z", lambda pos: here, lambda d: here, zr.at[h], "a1")

    def stage_a1(h):
        arrive(copies["a1", h])
        here = qf.at[h, y]
        copies["a2", h] = exchange("y", lambda pos: here, lambda d: here, yr.at[h], "a2")

    def stage_out(h):
        arrive(copies["a2", h])
        total = jnp.concatenate([qf[h, k] for k in range(PANELS)], axis=1)
        ut[h] = dot3(split(total), (wh[...], wl[...]))
        rows = pl.ds(h * CW, CW)
        here = part(x, CHIP)
        exchange("x", lambda pos: ut.at[h, part(pos, CW), :], lambda d: uin.at[rows, here], None, "out", back)
        uin[rows, here] = ut[h, part(x, CW), :]

    def stage_gc():
        arrive(copies["gc"])
        for p in range(NY):
            aq[p] = gp[pl.ds(pl.multiple_of(c * SHARE + p * AM, AM), AM), :] + gc[pl.ds(p * AM, AM), :]
        gb[...] = gp[pl.ds(pl.multiple_of(c * SHARE + HA, HB), HB), :] + gc[pl.ds(HA, HB), :]
        copies["r1", A] = exchange("y", lambda pos: aq.at[pos], lambda d: ayr.at[d - 1], ayr)
        copies["b1"] = exchange("z", lambda pos: gb.at[part(pos, BZ), :], lambda d: bzr.at[d - 1], bzr)

    def unit(pos):
        return pl.ds(pl.multiple_of(pos // 2 * 8, 8), 8), pl.ds(pl.multiple_of(pos % 2 * 128, 128), 128)

    def pairs_r1():
        arrive(copies["r1", A])
        ays[...] = added(aq[y], ayr)
        copies["r2", A] = exchange("z", lambda pos: ays.at[part(pos, AM // NZ), :], lambda d: azr.at[d - 1], azr)

    def pairs_r2():
        arrive(copies["r2", A])
        azs[...] = added(ays[part(z, AM // NZ), :], azr)
        copies["x", A] = exchange("x", lambda pos: azs.at[*unit(pos)], lambda d: axr.at[d - 1], axr)

    def pairs_x():
        arrive(copies["x", A])
        aqx[x, y, part(z, 8), :] = added(azs[*unit(x)], axr)
        here = aqx.at[x, y, part(z, 8), :]
        copies["a1", A] = exchange("z", lambda pos: here, lambda d: here, aqx.at[x, y, pl.ds(0, 8 * (NZ - 1)), :])

    def pairs_a1():
        arrive(copies["a1", A])
        here = aqx.at[x, y]
        copies["a2", A] = exchange("y", lambda pos: here, lambda d: here, aqx.at[x, pl.ds(0, NY - 1)])

    def pairs_a2():
        arrive(copies["a2", A])
        here = aqx.at[x]
        copies["a3", A] = exchange("x", lambda pos: here, lambda d: here, aqx.at[pl.ds(0, NX - 1)])

    spot = pl.ds(pl.multiple_of(c * SHARE + HA + z * BZ + y * BY, BY), BY)
    line = pl.ds(pl.multiple_of(c * SHARE + HA + z * BZ, BZ), BZ)

    def stage_b1():
        arrive(copies["b1"])
        bzs[...] = added(gb[part(z, BZ), :], bzr)
        copies["b2"] = exchange("y", lambda pos: bzs.at[part(pos, BY), :], lambda d: byr.at[d - 1], byr)

    def stage_b2():
        arrive(copies["b2"])
        bys[...] = added(bzs[part(y, BY), :], byr)
        copies["b3"] = exchange("x", lambda pos: bys, lambda d: bxr.at[d - 1], bxr)

    def stage_b3():
        arrive(copies["b3"])
        gf[spot, :] = added(bys[...], bxr)
        here = gf.at[spot, :]
        copies["b4"] = exchange("y", lambda pos: here, lambda d: here, byr)

    def stage_b4():
        arrive(copies["b4"])
        here = gf.at[line, :]
        copies["b5"] = exchange("z", lambda pos: here, lambda d: here, bzr)

    def stage_pairs():
        arrive(copies["a3", A])
        for p in range(NY):
            rows = pl.ds(pl.multiple_of(c * SHARE + p * AM, AM), AM)
            for lane in range(2):
                halves = jnp.stack([aqx[2 * half + lane, p].reshape(NZ, 8, 128) for half in range(2)], 1)
                gf[rows, pl.ds(lane * 128, 128)] = halves.reshape(AM, 128)
        here = gf.at[pl.ds(pl.multiple_of(c * SHARE, HB), HA), :]
        copies["gs"] = exchange("c", lambda pos: here, lambda d: here, here)

    def stage_b5():
        arrive(copies["b5"])
        here = gf.at[pl.ds(pl.multiple_of(c * SHARE + HA, HB), HB), :]
        copies["b6"] = exchange("c", lambda pos: here, lambda d: here, here)

    def fold(j):
        terms = {2: [(2, 3), (0, 3)], 1: [(1, 2), (1, 3)], 0: [(0, 1), (0, 2)]}[j]
        if j == 2:
            arrive(copies["b6"])
        if j == 1:
            arrive(copies["gs"])
        for target in sorted({term[0] for term in terms}):
            lines = pl.ds(target * WB, WB)
            total = wh[lines, :].astype(F32) + wl[lines, :].astype(F32)
            for k in [term[1] for term in terms if term[0] == target]:
                kl = pl.ds(k * WB, WB)
                pair = pl.ds(PAIRS.index((target, k)) * WB, WB)
                total = total - dot3(split(gf[pair, :]), (wh[kl, :], wl[kl, :]))
            wh[lines, :], wl[lines, :] = split(total)

    stages = {
        "next": send_in, "sib": prepare_sibling, "in": stage_in, "r1": stage_r1, "r2": stage_r2, "x": stage_x,
        "a1": stage_a1, "out": stage_out, "gc": stage_gc, "b1": stage_b1, "b2": stage_b2, "b3": stage_b3, "b4": stage_b4,
        "b5": stage_b5, "pairs": stage_pairs, "fold": fold,
    }
    pair_stages = {"r1": pairs_r1, "r2": pairs_r2, "x": pairs_x, "a1": pairs_a1, "a2": pairs_a2}
    for name, *which in ORDER:
        with jax.named_scope("_".join(map(str, [name, *which]))):
            if which == [A]:
                pair_stages[name]()
            else:
                stages[name](*which)

    stores = []

    def finish(pos):
        @pl.loop(0, CHIP // 512)
        def _(b):
            for u in range(4):
                rows = pl.ds(pl.multiple_of(pos * CHIP + b * 512 + u * 128, 128), 128)
                fv[rows, :] = fv[rows, :] - uin[:, rows].T

        store = pltpu.make_async_copy(fv.at[part(pos, CHIP), :], out_hbm.at[part(pos, CHIP), :], csem.at[len(stores)])
        store.start()
        stores.append(store)

    finish(x)
    for d in (1, 3, 2):
        pos = lax.rem(x + NX - d, NX)
        arrive((back[d], uin.at[:, part(pos, CHIP)]))
        finish(pos)
    all_in = fin.at[pl.ds(0, CH * (NX - 1) // NX)]
    totals = {"in": all_in, "out": all_in, "r1": yr, "r2": zr, "x": xr, "a1": zr, "a2": yr}
    for kind, (slot, whole) in sends.items():
        sent = totals.get(kind, whole)
        pltpu.make_async_copy(sent, sent, ssem.at[slot]).wait()
    for store in stores:
        store.wait()


SENDS, ARRIVALS = 22, NX - 1 + 6 * CH + 15


def body(eigvecs, reflectors, factors):
    def vm(*shape, dtype=F32):
        return pltpu.VMEM(shape, dtype)

    def half(*shape):
        return [vm(*shape, dtype=BF16)] * 2

    zrows, pairs = CM // NZ, len(PAIRS) * WB
    scratch = [
        vm(ROWS, COLS), vm(COLS, ROWS), vm(PANELS, OWN, WB), vm(PANELS, OWN, WB), vm(PANELS, WB, WB),
        *half(PANELS, WB, WB), *half(CHIP, WIDE), *half(WIDE, CHIP),
        vm(CH, CM, CHIP), vm(CH, PANELS, CM, WB), vm(CH, NY - 1, CM, WB), vm(CH, CM, WB), vm(CH, NZ - 1, zrows, WB),
        vm(CH, zrows, WB), vm(CH, NX - 1, zrows, WB), vm(CH, PANELS, CM, WB), vm(CH, CM, CHIP), vm(COLS, ROWS),
        vm(pairs, WB), vm(SHARE, WB), vm(NY, AM, WB), vm(NY - 1, AM, WB), vm(AM, WB), vm(NZ - 1, AM // NZ, WB),
        vm(AM // NZ, WB), vm(NX - 1, 8, 128), vm(NX, NY, NZ * 8, 128),
        vm(HB, WB), vm(NZ - 1, BZ, WB), vm(BZ, WB), vm(NY - 1, BY, WB), vm(BY, WB), vm(NX - 1, BY, WB),
        vm(pairs, WB),
        pltpu.SemaphoreType.DMA((3,)), pltpu.SemaphoreType.DMA((SENDS,)), pltpu.SemaphoreType.DMA((ARRIVALS,)),
        pltpu.SemaphoreType.DMA((NX,)),
    ]
    return pl.pallas_call(
        kernel,
        out_shape=jax.ShapeDtypeStruct((ROWS, COLS), F32),
        in_specs=[pl.BlockSpec(memory_space=pl.ANY)] * 3,
        out_specs=pl.BlockSpec(memory_space=pl.ANY),
        scratch_shapes=scratch,
        compiler_params=pltpu.CompilerParams(collective_id=0, has_side_effects=True, vmem_limit_bytes=63 * 2**20),
        name="back_transform",
    )(eigvecs, reflectors, factors)


def solution(mesh):
    in_specs = (P("row", "col"), P(None, ("row", "col"), None), P())
    return jax.shard_map(body, mesh=mesh, in_specs=in_specs, out_specs=P("row", "col"), check_vma=False)
```

time: 94.1 us -> 87.7 us (0.932)
  Pallas kernels: 91 us -> 84.5 us
    pallas_call x1, Pallas kernels: 91 us -> 84.5 us  [body(): pl.pallas_call(kernel, out_shape=jax.ShapeDtypeStruct((ROWS, COLS), F32),...]
where the time goes in v3:
time: 87.7 us; the launch traced here: 87.6 us
  Pallas kernels  84.5 us (96%)
  local copies, waits for them, and re-layouts  3.05 us (3%)
    pallas_call x1, Pallas kernels, body(): pl.pallas_call(kernel, out_shape=jax.ShapeDtypeStruct((ROWS, COLS), F32),...  84.5 us
    unnamed x1, local copies, waits for them, and re-layouts  3.05 us

profile of v3, /device:TPU:1, one launch (start us, length us, event | category | flops | bytes accessed | tf_op | source)
XLA Modules:
  0.0 87.6 jit_solution(4139163847785864655)
XLA Ops:
  0.0 84.5 %back_transform.1 = f32[4096,128]{1,0:T(8,128)} custom-call(f32[4096,128]{1,0:T(8,128)} %f_hbm.1, f32[4,512,256]{2,1,0:T(8,128)} %v_hbm.1, f32[4,256,256]{2,1,0:T(8,128)} %t_hbm.1), custom_call_target="tpu_custom_call" | custom-call | tf_op jit(solution)/shard_map/back_transform/pallas_call | solution.py:357
  84.5 3.0 %copy.5 = f32[4096,128]{1,0:T(8,128)} copy(f32[4096,128]{1,0:T(8,128)} %back_transform.1) | data formatting | bytes 4194304

commit v4 on v3

--- a/solution.py
+++ b/solution.py
@@ -360,7 +360,7 @@
         in_specs=[pl.BlockSpec(memory_space=pl.ANY)] * 3,
         out_specs=pl.BlockSpec(memory_space=pl.ANY),
         scratch_shapes=scratch,
-        compiler_params=pltpu.CompilerParams(collective_id=0, has_side_effects=True, vmem_limit_bytes=63 * 2**20),
+        compiler_params=pltpu.CompilerParams(collective_id=0, has_side_effects=True, vmem_limit_bytes=49 * 2**20),
         name="back_transform",
     )(eigvecs, reflectors, factors)
 

time: 87.7 us -> 86 us (0.981)
  Pallas kernels: 84.5 us -> 83.3 us
    pallas_call x1, Pallas kernels: 84.5 us -> 83.3 us  [body(): pl.pallas_call(kernel, out_shape=jax.ShapeDtypeStruct((ROWS, COLS), F32),...]
    unnamed x1 -> x3, local copies, waits for them, and re-layouts: 3.05 us -> 2.55 us
where the time goes in v4:
time: 86 us; the launch traced here: 85.9 us
  Pallas kernels  83.3 us (97%)
  local copies, waits for them, and re-layouts  2.55 us (3%)
    pallas_call x1, Pallas kernels, body(): pl.pallas_call(kernel, out_shape=jax.ShapeDtypeStruct((ROWS, COLS), F32),...  83.3 us
    unnamed x3, local copies, waits for them, and re-layouts  2.55 us

profile of v4, /device:TPU:1, one launch (start us, length us, event | category | flops | bytes accessed | tf_op | source)
XLA Modules:
  0.0 85.9 jit_solution(10083969367500716473)
XLA Ops:
  0.0 0.0 copy-start
  0.0 1.2 %copy-done = f32[4,256,256]{2,1,0:T(8,128)S(1)} copy-done((f32[4,256,256]{2,1,0:T(8,128)S(1)}, f32[4,256,256]{2,1,0:T(8,128)}, u32[]{:S(2)}) %copy-start) | copy-done | bytes 1048600
  1.2 83.3 %back_transform.1 = f32[4096,128]{1,0:T(8,128)S(1)} custom-call(f32[4096,128]{1,0:T(8,128)} %f_hbm.1, f32[4,512,256]{2,1,0:T(8,128)} %v_hbm.1, f32[4,256,256]{2,1,0:T(8,128)S(1)} %copy-done), custom_call_target="tpu_custom_call" | custom-call | tf_op jit(solution)/shard_map/back_transform/pallas_call | solution.py:357
  84.6 1.3 %copy.5 = f32[4096,128]{1,0:T(8,128)} copy(f32[4096,128]{1,0:T(8,128)S(1)} %back_transform.1) | data formatting | bytes 4194304
Async XLA Ops:
  0.0 1.2 %copy-start = (f32[4,256,256]{2,1,0:T(8,128)S(1)}, f32[4,256,256]{2,1,0:T(8,128)}, u32[]{:S(2)}) copy-start(f32[4,256,256]{2,1,0:T(8,128)} %t_hbm.1) | copy-start | bytes 3145732

commit v5 on v4

--- a/solution.py
+++ b/solution.py
@@ -27,13 +27,13 @@
 BZ, BY = HB // NZ, HB // NZ // NY
 A = CH
 ORDER = [
-    ("next", 1), ("next", 2), ("next", 3), ("next", 4), ("gc",), ("sib",), ("in", 0), ("in", 1), ("r1", A), ("in", 2), ("b1",),
-    ("r1", 0), ("in", 3), ("next", 5), ("r1", 1), ("in", 4), ("r2", A), ("b2",), ("r1", 2), ("r2", 0), ("next", 6), ("next", 7),
-    ("x", A), ("b3",), ("r1", 3), ("in", 5), ("x", 0), ("r2", 1), ("r1", 4), ("a1", A), ("r2", 2), ("b4",), ("in", 6), ("in", 7),
-    ("r2", 3), ("x", 1), ("a1", 0), ("a2", A), ("r1", 5), ("r1", 6), ("x", 2), ("r2", 4), ("b5",), ("r1", 7), ("x", 3), ("a1", 1),
-    ("fold", 2), ("r2", 5), ("pairs",), ("r2", 6), ("x", 4), ("fold", 1), ("x", 5), ("a1", 2), ("fold", 0), ("out", 0), ("r2", 7),
-    ("x", 6), ("a1", 3), ("out", 1), ("a1", 4), ("out", 2), ("a1", 6), ("x", 7), ("a1", 5), ("out", 3), ("out", 4), ("a1", 7),
-    ("out", 6), ("out", 5), ("out", 7),
+    ("next", 1), ("gc",), ("next", 2), ("sib",), ("next", 3), ("in", 0), ("next", 4), ("in", 1), ("b1",), ("r1", A), ("next", 5),
+    ("in", 2), ("r1", 0), ("in", 4), ("r2", A), ("b2",), ("r1", 1), ("r2", 0), ("next", 6), ("x", A), ("b3",), ("r1", 2),
+    ("x", 0), ("in", 5), ("r2", 1), ("r1", 4), ("next", 7), ("b4",), ("a1", A), ("x", 1), ("in", 3), ("r2", 2), ("in", 6),
+    ("in", 7), ("r2", 4), ("r1", 5), ("a2", A), ("a1", 0), ("x", 2), ("r1", 3), ("b5",), ("r1", 6), ("x", 4), ("a1", 1),
+    ("r2", 5), ("pairs",), ("fold", 2), ("r1", 7), ("a1", 2), ("fold", 1), ("r2", 3), ("x", 5), ("fold", 0), ("r2", 6),
+    ("out", 0), ("a1", 4), ("x", 3), ("r2", 7), ("out", 1), ("a1", 5), ("x", 6), ("out", 2), ("x", 7), ("a1", 3), ("out", 4),
+    ("a1", 6), ("a1", 7), ("out", 5), ("out", 3), ("out", 6), ("out", 7),
 ]
 
 
@@ -86,7 +86,7 @@
         if recv is None:
             recv = [arrivals[0]] * SIZES[axis]
             arrivals[0] += 1
-        for d in range(1, SIZES[axis]):
+        for d in sorted(range(1, SIZES[axis]), key=lambda d: -min(d, SIZES[axis] - d)):
             pos, peer = along(axis, d)
             pltpu.make_async_remote_copy(
                 src_ref=source(pos), dst_ref=target(d), send_sem=ssem.at[slot], recv_sem=rsem.at[recv[d]],
@@ -277,19 +277,14 @@
         copies["b6"] = exchange("c", lambda pos: here, lambda d: here, here)
 
     def fold(j):
-        terms = {2: [(2, 3), (0, 3)], 1: [(1, 2), (1, 3)], 0: [(0, 1), (0, 2)]}[j]
-        if j == 2:
-            arrive(copies["b6"])
-        if j == 1:
-            arrive(copies["gs"])
-        for target in sorted({term[0] for term in terms}):
-            lines = pl.ds(target * WB, WB)
+        if j:
+            arrive(copies["b6" if j == 2 else "gs"])
+        for target, first, last in {2: [(2, 3, 3), (0, 3, 3)], 1: [(1, 2, 3)], 0: [(0, 1, 2)]}[j]:
+            lines, others = pl.ds(target * WB, WB), pl.ds(first * WB, (last + 1 - first) * WB)
+            blocks = [gf[pl.ds(PAIRS.index((target, k)) * WB, WB), :] for k in range(first, last + 1)]
             total = wh[lines, :].astype(F32) + wl[lines, :].astype(F32)
-            for k in [term[1] for term in terms if term[0] == target]:
-                kl = pl.ds(k * WB, WB)
-                pair = pl.ds(PAIRS.index((target, k)) * WB, WB)
-                total = total - dot3(split(gf[pair, :]), (wh[kl, :], wl[kl, :]))
-            wh[lines, :], wl[lines, :] = split(total)
+            taken = dot3(split(jnp.concatenate(blocks, axis=1)), (wh[others, :], wl[others, :]))
+            wh[lines, :], wl[lines, :] = split(total - taken)
 
     stages = {
         "next": send_in, "sib": prepare_sibling, "in": stage_in, "r1": stage_r1, "r2": stage_r2, "x": stage_x,

time: 86 us -> 84.4 us (0.981)
  Pallas kernels: 83.3 us -> 81.3 us
    pallas_call x1, Pallas kernels: 83.3 us -> 81.3 us  [body(): pl.pallas_call(kernel, out_shape=jax.ShapeDtypeStruct((ROWS, COLS), F32),...]
where the time goes in v5:
time: 84.4 us; the launch traced here: 83.8 us
  Pallas kernels  81.3 us (96%)
  local copies, waits for them, and re-layouts  2.55 us (3%)
    pallas_call x1, Pallas kernels, body(): pl.pallas_call(kernel, out_shape=jax.ShapeDtypeStruct((ROWS, COLS), F32),...  81.3 us
    unnamed x3, local copies, waits for them, and re-layouts  2.55 us

profile of v5, /device:TPU:1, one launch (start us, length us, event | category | flops | bytes accessed | tf_op | source)
XLA Modules:
  0.0 83.8 jit_solution(8875725745683991207)
XLA Ops:
  0.0 0.0 copy-start
  0.0 1.2 %copy-done = f32[4,256,256]{2,1,0:T(8,128)S(1)} copy-done((f32[4,256,256]{2,1,0:T(8,128)S(1)}, f32[4,256,256]{2,1,0:T(8,128)}, u32[]{:S(2)}) %copy-start) | copy-done | bytes 1048600
  1.2 81.3 %back_transform.1 = f32[4096,128]{1,0:T(8,128)S(1)} custom-call(f32[4096,128]{1,0:T(8,128)} %f_hbm.1, f32[4,512,256]{2,1,0:T(8,128)} %v_hbm.1, f32[4,256,256]{2,1,0:T(8,128)S(1)} %copy-done), custom_call_target="tpu_custom_call" | custom-call | tf_op jit(solution)/shard_map/back_transform/pallas_call | solution.py:352
  82.5 1.3 %copy.5 = f32[4096,128]{1,0:T(8,128)} copy(f32[4096,128]{1,0:T(8,128)S(1)} %back_transform.1) | data formatting | bytes 4194304
Async XLA Ops:
  0.0 1.2 %copy-start = (f32[4,256,256]{2,1,0:T(8,128)S(1)}, f32[4,256,256]{2,1,0:T(8,128)}, u32[]{:S(2)}) copy-start(f32[4,256,256]{2,1,0:T(8,128)} %t_hbm.1) | copy-start | bytes 3145732

commit v6 on v5

--- a/solution.py
+++ b/solution.py
@@ -313,7 +313,7 @@
         stores.append(store)
 
     finish(x)
-    for d in (1, 3, 2):
+    for d in (2, 1, 3):
         pos = lax.rem(x + NX - d, NX)
         arrive((back[d], uin.at[:, part(pos, CHIP)]))
         finish(pos)

time: 84.4 us -> 84.1 us (level)
  no operation moved by 1% of the time
where the time goes in v6:
time: 84.1 us; the launch traced here: 83.5 us
  Pallas kernels  81 us (96%)
  local copies, waits for them, and re-layouts  2.55 us (3%)
    pallas_call x1, Pallas kernels, body(): pl.pallas_call(kernel, out_shape=jax.ShapeDtypeStruct((ROWS, COLS), F32),...  81 us
    unnamed x3, local copies, waits for them, and re-layouts  2.55 us

profile of v6, /device:TPU:1, one launch (start us, length us, event | category | flops | bytes accessed | tf_op | source)
XLA Modules:
  0.0 83.5 jit_solution(6504354137796353252)
XLA Ops:
  0.0 0.0 copy-start
  0.0 1.2 %copy-done = f32[4,256,256]{2,1,0:T(8,128)S(1)} copy-done((f32[4,256,256]{2,1,0:T(8,128)S(1)}, f32[4,256,256]{2,1,0:T(8,128)}, u32[]{:S(2)}) %copy-start) | copy-done | bytes 1048600
  1.2 81.0 %back_transform.1 = f32[4096,128]{1,0:T(8,128)S(1)} custom-call(f32[4096,128]{1,0:T(8,128)} %f_hbm.1, f32[4,512,256]{2,1,0:T(8,128)} %v_hbm.1, f32[4,256,256]{2,1,0:T(8,128)S(1)} %copy-done), custom_call_target="tpu_custom_call" | custom-call | tf_op jit(solution)/shard_map/back_transform/pallas_call | solution.py:352
  82.2 1.3 %copy.5 = f32[4096,128]{1,0:T(8,128)} copy(f32[4096,128]{1,0:T(8,128)S(1)} %back_transform.1) | data formatting | bytes 4194304
Async XLA Ops:
  0.0 1.2 %copy-start = (f32[4,256,256]{2,1,0:T(8,128)S(1)}, f32[4,256,256]{2,1,0:T(8,128)}, u32[]{:S(2)}) copy-start(f32[4,256,256]{2,1,0:T(8,128)} %t_hbm.1) | copy-start | bytes 3145732
